TPU v7x, 32 devices: a whole 2x2x4 slice. The times are simulated.
32 devices in a mesh: gx: 2 (over x), gy: 4 (over z), gz: 4 (over y, core).
Axes of the slice: x: 2, y: 2, z: 4, core: 2. Of those that a mesh axis runs over, the one named last changes fastest.
Arguments:
- acts: bfloat16 [40960, 768], P(('gx', 'gy', 'gz')), may hold values from -6 to 6
- grads_out: bfloat16 [40960, 768], P(('gx', 'gy', 'gz')), may hold values from -0.03125 to 0.03125
- master: float32 [4608, 128], P(('gx', 'gy', 'gz')), may hold values from -0.3 to 0.3
- moment: float32 [4608, 128], P(('gx', 'gy', 'gz')), may hold values from -6 to 6
- second: float32 [4608, 128], P(('gx', 'gy', 'gz')), may hold values from 0.1 to 2
Outputs:
- master_new: float32 [4608, 128], P(('gx', 'gy', 'gz'))
- moment_new: float32 [4608, 128], P(('gx', 'gy', 'gz'))
- second_new: float32 [4608, 128], P(('gx', 'gy', 'gz'))
- weights: bfloat16 [768, 768], replicated
All inputs are finite; a program needn't handle non-finite values.
Results may differ from a plain program's by a relative error of at most 0.003.
Values may be sent and summed in bfloat16 or wider, within the bound.
No kernel may reach another device: no remote copies, remote signals or barrier semaphores. Data moves between devices by JAX's collectives and lax.ppermute only.
A program may use at most 64 MiB of HBM per device.

v0:
```python
import jax
import jax.numpy as jnp
from jax import lax
from jax.sharding import PartitionSpec as P

STEP = 1000


def shards(acts, grads_out, master, moment, second):
    width_in = acts.shape[1]
    width_out = grads_out.shape[1]
    lane = master.shape[1]
    total_rows = width_in * width_out // lane
    local_grad = lax.dot_general(
        acts, grads_out, (((0,), (0,)), ((), ())), preferred_element_type=jnp.float32
    )
    local_flat = local_grad.reshape(total_rows, lane)
    partial_value = lax.psum_scatter(
        local_flat.astype(jnp.bfloat16), "gx", scatter_dimension=0, tiled=True
    ).astype(jnp.float32)
    partial_value = lax.psum_scatter(
        partial_value.astype(jnp.bfloat16), "gy", scatter_dimension=0, tiled=True
    ).astype(jnp.float32)
    gradient = lax.psum_scatter(
        partial_value.astype(jnp.bfloat16), "gz", scatter_dimension=0, tiled=True
    ).astype(jnp.float32)
    moment_new = 0.9 * moment + 0.1 * gradient
    second_new = 0.95 * second + 0.05 * gradient * gradient
    first_fix = 1.0 - 0.9**STEP
    second_fix = 1.0 - 0.95**STEP
    ratio = moment_new / first_fix / (jnp.sqrt(second_new / second_fix) + 1e-08)
    master_new = master - 0.01 * (ratio + 0.01 * master)
    rounded = master_new.astype(jnp.bfloat16)
    gathered = lax.all_gather(rounded, "gz", axis=0, tiled=True)
    gathered = lax.all_gather(gathered, "gy", axis=0, tiled=True)
    gathered = lax.all_gather(gathered, "gx", axis=0, tiled=True)
    weights = gathered.reshape(width_in, width_out)
    return (master_new, moment_new, second_new, weights)


def solution(mesh):
    return jax.shard_map(
        shards,
        mesh=mesh,
        in_specs=(
            P(("gx", "gy", "gz"), None),
            P(("gx", "gy", "gz"), None),
            P(("gx", "gy", "gz"), None),
            P(("gx", "gy", "gz"), None),
            P(("gx", "gy", "gz"), None),
        ),
        out_specs=(
            P(("gx", "gy", "gz"), None),
            P(("gx", "gy", "gz"), None),
            P(("gx", "gy", "gz"), None),
            P(),
        ),
        check_vma=False,
    )
```

profile of v0, /device:TPU:0, one launch (start us, length us, event | category | flops | bytes accessed | tf_op | source)
XLA Modules:
  0.0 141.0 jit_solution(13236243267090482629)
XLA Ops:
  7.2 0.0 copy-start
  7.2 0.0 reduce-scatter.4.cloned.1.call-start
  7.2 1.5 %copy-done = bf16[1280,768]{1,0:T(8,128)(2,1)S(1)} copy-done((bf16[1280,768]{1,0:T(8,128)(2,1)S(1)}, bf16[1280,768]{1,0:T(8,128)(2,1)}, u32[]{:S(2)}) %copy-start) | copy-done | bytes 1966104
  8.7 3.3 %convolution_convert_fusion = bf16[768,768]{1,0:T(8,128)(2,1)S(1)} fusion(bf16[1280,768]{1,0:T(8,128)(2,1)S(1)} %copy-done, bf16[1280,768]{1,0:T(8,128)(2,1)} %param.6), kind=kOutput, calls=%fused_computation | convolution fusion | flops 1510539264 | bytes 5111808 | tf_op jit(solution)/shard_map/dot_general | solution.py:14
  12.0 0.0 copy-start.1
  12.0 0.0 copy-start.2
  12.0 0.0 copy-start.3
  12.1 1.9 %convert_element_type.17 = bf16[4608,128]{1,0:T(8,128)(2,1)} reshape(bf16[768,768]{1,0:T(8,128)(2,1)S(1)} %convolution_convert_fusion) | data formatting | bytes 2359296 | tf_op jit(solution)/shard_map/convert_element_type | solution.py:19
  13.9 0.0 reduce-scatter.4.cloned.1.call-update
  13.9 0.0 reduce-scatter.6.cloned.1.call-start
  14.0 24.7 %reduce-scatter.4.cloned.1.call-done = bf16[2304,128]{1,0:T(8,128)(2,1)} async-done(((bf16[4608,128]{1,0:T(8,128)(2,1)}), bf16[2304,128]{1,0:T(8,128)(2,1)}) %reduce-scatter.4.cloned.1.call-update) | async-done | bytes 589840 | tf_op jit(solution)/shard_map/reduce_scatter | solution.py:18
  38.7 0.0 reduce-scatter.6.cloned.1.call-update
  38.7 0.0 reduce-scatter.8.cloned.1.call-start
  38.7 24.4 %reduce-scatter.6.cloned.1.call-done = bf16[576,128]{1,0:T(8,128)(2,1)} async-done(((bf16[2304,128]{1,0:T(8,128)(2,1)}), bf16[576,128]{1,0:T(8,128)(2,1)}) %reduce-scatter.6.cloned.1.call-update) | async-done | bytes 147472 | tf_op jit(solution)/shard_map/reduce_scatter | solution.py:21
  63.1 0.0 reduce-scatter.8.cloned.1.call-update
  63.1 0.0 all-gather.2.cloned.1.call-start
  63.2 20.5 %reduce-scatter.8.cloned.1.call-done = bf16[144,128]{1,0:T(8,128)(2,1)} async-done(((bf16[576,128]{1,0:T(8,128)(2,1)}), bf16[144,128]{1,0:T(8,128)(2,1)}) %reduce-scatter.8.cloned.1.call-update) | async-done | bytes 36880 | tf_op jit(solution)/shard_map/reduce_scatter | solution.py:24
  83.7 0.0 copy-done.1
  83.7 1.5 %fusion.2 = (bf16[144,128]{1,0:T(8,128)(2,1)S(1)}, f32[144,128]{1,0:T(8,128)}, f32[144,128]{1,0:T(8,128)}, f32[144,128]{1,0:T(8,128)}) fusion(f32[144,128]{1,0:T(8,128)S(1)} %copy-done.1, bf16[144,128]{1,0:T(8,128)(2,1)} %reduce-scatter.8.cloned.1.call-done, f32[144,128]{1,0:T(8,128)S(1)} %copy-done.2, f32[144,128]{1,0:T(8,128)S(1)} %copy-done.3), kind=kLoop, calls=%fused_computation.6 | loop fusion | flops 276480 | bytes 516096 | tf_op jit(solution)/shard_map/convert_element_type | solution.py:33
  85.2 5.4 %all_gather.9 = bf16[576,128]{1,0:T(8,128)(2,1)S(1)} all-gather(bf16[144,128]{1,0:T(8,128)(2,1)S(1)} %get-tuple-element.4), channel_id=1, replica_groups=mesh['gx'=2,'gy'=4,'gz'=4] {'gz'}, dimensions={0}, use_global_device_ids=true | all-gather | bytes 184320 | tf_op jit(solution)/shard_map/all_gather | solution.py:34
  90.6 17.2 %all_gather.10 = bf16[2304,128]{1,0:T(8,128)(2,1)} all-gather(bf16[576,128]{1,0:T(8,128)(2,1)S(1)} %all_gather.9), channel_id=1, replica_groups=mesh['gx'=2,'gy'=4,'gz'=4] {'gy'}, dimensions={0}, use_global_device_ids=true | all-gather | bytes 737280 | tf_op jit(solution)/shard_map/all_gather | solution.py:35
  107.8 0.0 all-gather.2.cloned.1.call-update
  107.8 23.3 %all-gather.2.cloned.1.call-done = bf16[4608,128]{1,0:T(8,128)(2,1)} async-done(((bf16[2304,128]{1,0:T(8,128)(2,1)}), bf16[4608,128]{1,0:T(8,128)(2,1)}) %all-gather.2.cloned.1.call-update) | async-done | bytes 1179664 | tf_op jit(solution)/shard_map/all_gather | solution.py:36
  131.1 3.3 %reshape.13 = bf16[768,768]{1,0:T(8,128)(2,1)} reshape(bf16[4608,128]{1,0:T(8,128)(2,1)} %all-gather.2.cloned.1.call-done) | data formatting | bytes 2359296 | tf_op jit(solution)/shard_map/reshape | solution.py:37
  (2 shorter events, 0.0 us)
Async XLA Ops:
  7.2 1.6 %copy-start = (bf16[1280,768]{1,0:T(8,128)(2,1)S(1)}, bf16[1280,768]{1,0:T(8,128)(2,1)}, u32[]{:S(2)}) copy-start(bf16[1280,768]{1,0:T(8,128)(2,1)} %param.5) | copy-start | bytes 5898244
  7.2 31.5 %reduce-scatter.4.cloned.1.call-start = ((), (), s32[]{:S(2)}) async-start(), calls=%async_computation.3 | async-start | bytes 1769472 | tf_op jit(solution)/shard_map/reduce_scatter | solution.py:18
  12.0 71.7 %copy-start.1 = (f32[144,128]{1,0:T(8,128)S(1)}, f32[144,128]{1,0:T(8,128)}, u32[]{:S(2)}) copy-start(f32[144,128]{1,0:T(8,128)} %param.7) | copy-start | bytes 221188
  12.0 71.7 %copy-start.2 = (f32[144,128]{1,0:T(8,128)S(1)}, f32[144,128]{1,0:T(8,128)}, u32[]{:S(2)}) copy-start(f32[144,128]{1,0:T(8,128)} %param.9) | copy-start | bytes 221188
  12.0 71.7 %copy-start.3 = (f32[144,128]{1,0:T(8,128)S(1)}, f32[144,128]{1,0:T(8,128)}, u32[]{:S(2)}) copy-start(f32[144,128]{1,0:T(8,128)} %param.8) | copy-start | bytes 221188
  13.9 49.2 %reduce-scatter.6.cloned.1.call-start = ((), (), s32[]{:S(2)}) async-start(), calls=%async_computation.4 | async-start | bytes 737280 | tf_op jit(solution)/shard_map/reduce_scatter | solution.py:21
  38.7 45.0 %reduce-scatter.8.cloned.1.call-start = ((), (), s32[]{:S(2)}) async-start(), calls=%async_computation.5 | async-start | bytes 184320 | tf_op jit(solution)/shard_map/reduce_scatter | solution.py:24
  63.1 68.0 %all-gather.2.cloned.1.call-start = ((), (), s32[]{:S(2)}) async-start(), calls=%async_computation.6 | async-start | bytes 1769472 | tf_op jit(solution)/shard_map/all_gather | solution.py:36
Sparse Core Ops, SparseCore 0:
  14.1 24.5 reduce-scatter.3
  40.9 22.1 reduce-scatter.5
  65.5 18.1 reduce-scatter.7
  108.0 23.0 all-gather.1
where the time goes:
time: 141 us
  waiting for transfers between devices  92.9 us (66%)
  blocking collectives  22.6 us (16%)
  between operations  13.8 us (10%)
  local copies, waits for them, and re-layouts  6.73 us (5%)
  matrix products  3.29 us (2%)
  other arithmetic  1.48 us (1%)
    reduce_scatter x1, waiting for transfers between devices, shards(): lax.psum_scatter(local_flat.astype(jnp.bfloat16), 'gx', scatter_dimension...  24.7 us
    reduce_scatter x1, waiting for transfers between devices, shards(): lax.psum_scatter(partial_value.astype(jnp.bfloat16), 'gy', scatter_dimens...  24.4 us
    all_gather x1, waiting for transfers between devices, shards(): gathered = lax.all_gather(gathered, 'gx', axis=0, tiled=True)  23.3 us
    reduce_scatter x1, waiting for transfers between devices, shards(): lax.psum_scatter(partial_value.astype(jnp.bfloat16), 'gz', scatter_dimens...  20.5 us
    all_gather x1, blocking collectives, shards(): gathered = lax.all_gather(gathered, 'gy', axis=0, tiled=True)  17.2 us
    all_gather x1, blocking collectives, shards(): gathered = lax.all_gather(rounded, 'gz', axis=0, tiled=True)  5.45 us
    reshape x1, local copies, waits for them, and re-layouts, shards(): weights = gathered.reshape(width_in, width_out)  3.35 us
    dot_general x1, matrix products, shards(): lax.dot_general(acts, grads_out, (((0,), (0,)), ((), ())), preferred_elem...  3.29 us
  transfers between devices with their start and end apart: 4, of which 4 were waited for; matrix products, arithmetic and copies ran while one was open for 0% of the time, Pallas kernels for 0%

commit v1 on v0

--- a/solution.py
+++ b/solution.py
@@ -33,7 +33,9 @@
     rounded = master_new.astype(jnp.bfloat16)
     gathered = lax.all_gather(rounded, "gz", axis=0, tiled=True)
     gathered = lax.all_gather(gathered, "gy", axis=0, tiled=True)
-    gathered = lax.all_gather(gathered, "gx", axis=0, tiled=True)
+    gathered = jnp.concatenate(
+        lax.all_to_all(jnp.stack([gathered] * lax.axis_size("gx"), axis=0), "gx", 0, 0), 0
+    )
     weights = gathered.reshape(width_in, width_out)
     return (master_new, moment_new, second_new, weights)
 

time: 141 us -> 133 us (0.943)
  waiting for transfers between devices: 92.9 us -> 69.7 us
  blocking collectives: 22.6 us -> 38.7 us
  local copies, waits for them, and re-layouts: 6.73 us -> 5.23 us
    all_gather x1 -> x0, waiting for transfers between devices: 23.3 us -> none  [shards(): gathered = lax.all_gather(gathered, 'gx', axis=0, tiled=True)]
    all_to_all x0 -> x1, blocking collectives: none -> 15.9 us  [shards(): lax.all_to_all(jnp.stack([gathered] * lax.axis_size('gx'), axis=0), 'gx',...]
    reshape x1 -> x0, local copies, waits for them, and re-layouts: 3.35 us -> none  [shards(): weights = gathered.reshape(width_in, width_out)]
    another operation x0 -> x1, local copies, waits for them, and re-layouts: none -> 1.85 us  [shards(): weights = gathered.reshape(width_in, width_out)]
  transfers between devices with their start and end apart: 4 -> 3, of which waited for: 4 -> 3; matrix products, arithmetic and copies ran while one was open for 0% -> 0% of each run, Pallas kernels for 0% -> 0%
where the time goes in v1:
time: 133 us; the launch traced here: 132 us
  waiting for transfers between devices  69.7 us (52%)
  blocking collectives  38.7 us (29%)
  between operations  13.8 us (10%)
  local copies, waits for them, and re-layouts  5.23 us (4%)
  matrix products  3.29 us (2%)
  other arithmetic  1.58 us (1%)
    reduce_scatter x1, waiting for transfers between devices, shards(): lax.psum_scatter(local_flat.astype(jnp.bfloat16), 'gx', scatter_dimension...  24.7 us
    reduce_scatter x1, waiting for transfers between devices, shards(): lax.psum_scatter(partial_value.astype(jnp.bfloat16), 'gy', scatter_dimens...  24.4 us
    reduce_scatter x1, waiting for transfers between devices, shards(): lax.psum_scatter(partial_value.astype(jnp.bfloat16), 'gz', scatter_dimens...  20.6 us
    all_gather x1, blocking collectives, shards(): gathered = lax.all_gather(gathered, 'gy', axis=0, tiled=True)  17.3 us
    all_to_all x1, blocking collectives, shards(): lax.all_to_all(jnp.stack([gathered] * lax.axis_size('gx'), axis=0), 'gx',...  15.9 us
    all_gather x1, blocking collectives, shards(): gathered = lax.all_gather(rounded, 'gz', axis=0, tiled=True)  5.45 us
    dot_general x1, matrix products, shards(): lax.dot_general(acts, grads_out, (((0,), (0,)), ((), ())), preferred_elem...  3.29 us
  transfers between devices with their start and end apart: 3, of which 3 were waited for; matrix products, arithmetic and copies ran while one was open for 0% of the time, Pallas kernels for 0%

profile of v1, /device:TPU:0, one launch (start us, length us, event | category | flops | bytes accessed | tf_op | source)
XLA Modules:
  0.0 132.3 jit_solution(4567253798917820112)
XLA Ops:
  7.2 0.0 copy-start
  7.2 0.0 reduce-scatter.4.cloned.1.call-start
  7.2 1.5 %copy-done = bf16[1280,768]{1,0:T(8,128)(2,1)S(1)} copy-done((bf16[1280,768]{1,0:T(8,128)(2,1)S(1)}, bf16[1280,768]{1,0:T(8,128)(2,1)}, u32[]{:S(2)}) %copy-start) | copy-done | bytes 1966104
  8.7 3.3 %convolution_convert_fusion = bf16[768,768]{1,0:T(8,128)(2,1)S(1)} fusion(bf16[1280,768]{1,0:T(8,128)(2,1)S(1)} %copy-done, bf16[1280,768]{1,0:T(8,128)(2,1)} %param.6), kind=kOutput, calls=%fused_computation | convolution fusion | flops 1510539264 | bytes 5111808 | tf_op jit(solution)/shard_map/dot_general | solution.py:14
  12.0 0.0 copy-start.1
  12.0 0.0 copy-start.2
  12.0 0.0 copy-start.3
  12.1 1.9 %convert_element_type.17 = bf16[4608,128]{1,0:T(8,128)(2,1)} reshape(bf16[768,768]{1,0:T(8,128)(2,1)S(1)} %convolution_convert_fusion) | data formatting | bytes 2359296 | tf_op jit(solution)/shard_map/convert_element_type | solution.py:19
  13.9 0.0 reduce-scatter.4.cloned.1.call-update
  13.9 0.0 reduce-scatter.6.cloned.1.call-start
  14.0 24.7 %reduce-scatter.4.cloned.1.call-done = bf16[2304,128]{1,0:T(8,128)(2,1)} async-done(((bf16[4608,128]{1,0:T(8,128)(2,1)}), bf16[2304,128]{1,0:T(8,128)(2,1)}) %reduce-scatter.4.cloned.1.call-update) | async-done | bytes 589840 | tf_op jit(solution)/shard_map/reduce_scatter | solution.py:18
  38.7 0.0 reduce-scatter.6.cloned.1.call-update
  38.7 0.0 reduce-scatter.8.cloned.1.call-start
  38.7 24.4 %reduce-scatter.6.cloned.1.call-done = bf16[576,128]{1,0:T(8,128)(2,1)} async-done(((bf16[2304,128]{1,0:T(8,128)(2,1)}), bf16[576,128]{1,0:T(8,128)(2,1)}) %reduce-scatter.6.cloned.1.call-update) | async-done | bytes 147472 | tf_op jit(solution)/shard_map/reduce_scatter | solution.py:21
  63.1 0.0 reduce-scatter.8.cloned.1.call-update
  63.1 20.6 %reduce-scatter.8.cloned.1.call-done = bf16[144,128]{1,0:T(8,128)(2,1)} async-done(((bf16[576,128]{1,0:T(8,128)(2,1)}), bf16[144,128]{1,0:T(8,128)(2,1)}) %reduce-scatter.8.cloned.1.call-update) | async-done | bytes 36880 | tf_op jit(solution)/shard_map/reduce_scatter | solution.py:24
  83.7 0.0 copy-done.1
  83.7 0.0 copy-done.2
  83.7 1.5 %fusion.2 = (bf16[144,128]{1,0:T(8,128)(2,1)S(1)}, f32[144,128]{1,0:T(8,128)}, f32[144,128]{1,0:T(8,128)}, f32[144,128]{1,0:T(8,128)}) fusion(f32[144,128]{1,0:T(8,128)S(1)} %copy-done.1, bf16[144,128]{1,0:T(8,128)(2,1)} %reduce-scatter.8.cloned.1.call-done, f32[144,128]{1,0:T(8,128)S(1)} %copy-done.2, f32[144,128]{1,0:T(8,128)S(1)} %copy-done.3), kind=kLoop, calls=%fused_computation.7 | loop fusion | flops 276480 | bytes 516096 | tf_op jit(solution)/shard_map/convert_element_type | solution.py:33
  85.2 5.4 %all_gather.6 = bf16[576,128]{1,0:T(8,128)(2,1)S(1)} all-gather(bf16[144,128]{1,0:T(8,128)(2,1)S(1)} %get-tuple-element.4), channel_id=1, replica_groups=mesh['gx'=2,'gy'=4,'gz'=4] {'gz'}, dimensions={0}, use_global_device_ids=true | all-gather | bytes 184320 | tf_op jit(solution)/shard_map/all_gather | solution.py:34
  90.6 17.3 %all_gather.7 = bf16[2304,128]{1,0:T(8,128)(2,1)S(1)} all-gather(bf16[576,128]{1,0:T(8,128)(2,1)S(1)} %all_gather.6), channel_id=1, replica_groups=mesh['gx'=2,'gy'=4,'gz'=4] {'gy'}, dimensions={0}, use_global_device_ids=true | all-gather | bytes 737280 | tf_op jit(solution)/shard_map/all_gather | solution.py:35
  107.9 0.1 pad_maximum_fusion
  108.0 15.9 %all_to_all.5 = bf16[2,2304,128]{2,1,0:T(8,128)(2,1)S(1)} all-to-all(bf16[2,2304,128]{2,1,0:T(8,128)(2,1)S(1)} %pad_maximum_fusion), channel_id=1, replica_groups=mesh['gx'=2,'gy'=4,'gz'=4] {'gx'}, dimensions={0} | all-to-all | bytes 2359296 | tf_op jit(solution)/shard_map/all_to_all | solution.py:37
  123.9 1.9 %reshape_reshape.3 = bf16[768,768]{1,0:T(8,128)(2,1)} reshape(bf16[2,2304,128]{2,1,0:T(8,128)(2,1)S(1)} %all_to_all.5) | data formatting | bytes 2359296 | tf_op jit(solution)/shard_map/reshape;reshape | solution.py:39
  (1 shorter events, 0.0 us)
Async XLA Ops:
  7.2 1.6 %copy-start = (bf16[1280,768]{1,0:T(8,128)(2,1)S(1)}, bf16[1280,768]{1,0:T(8,128)(2,1)}, u32[]{:S(2)}) copy-start(bf16[1280,768]{1,0:T(8,128)(2,1)} %param.5) | copy-start | bytes 5898244
  7.2 31.5 %reduce-scatter.4.cloned.1.call-start = ((), (), s32[]{:S(2)}) async-start(), calls=%async_computation.4 | async-start | bytes 1769472 | tf_op jit(solution)/shard_map/reduce_scatter | solution.py:18
  12.0 71.7 %copy-start.1 = (f32[144,128]{1,0:T(8,128)S(1)}, f32[144,128]{1,0:T(8,128)}, u32[]{:S(2)}) copy-start(f32[144,128]{1,0:T(8,128)} %param.7) | copy-start | bytes 221188
  12.0 71.7 %copy-start.2 = (f32[144,128]{1,0:T(8,128)S(1)}, f32[144,128]{1,0:T(8,128)}, u32[]{:S(2)}) copy-start(f32[144,128]{1,0:T(8,128)} %param.9) | copy-start | bytes 221188
  12.0 71.7 %copy-start.3 = (f32[144,128]{1,0:T(8,128)S(1)}, f32[144,128]{1,0:T(8,128)}, u32[]{:S(2)}) copy-start(f32[144,128]{1,0:T(8,128)} %param.8) | copy-start | bytes 221188
  13.9 49.2 %reduce-scatter.6.cloned.1.call-start = ((), (), s32[]{:S(2)}) async-start(), calls=%async_computation.5 | async-start | bytes 737280 | tf_op jit(solution)/shard_map/reduce_scatter | solution.py:21
  38.7 45.0 %reduce-scatter.8.cloned.1.call-start = ((), (), s32[]{:S(2)}) async-start(), calls=%async_computation.6 | async-start | bytes 184320 | tf_op jit(solution)/shard_map/reduce_scatter | solution.py:24
Sparse Core Ops, SparseCore 0:
  14.1 24.5 reduce-scatter.3
  40.9 22.1 reduce-scatter.5
  65.5 18.1 reduce-scatter.7
